TPU v7x, 32 devices: a whole 2x2x4 slice. The times are simulated.
32 devices in a mesh: rep: 4 (over x, core), mx: 2 (over y), my: 4 (over z).
Axes of the slice: x: 2, y: 2, z: 4, core: 2. Of those that a mesh axis runs over, the one named last changes fastest.
Arguments:
- coefficients: bfloat16 [2, 384, 384, 384], P(None, 'mx', 'my'), may hold values from -7.5 to 7.5
- noise_field: bfloat16 [128, 2, 1536, 1536], P(('rep', 'mx'), None, 'my'), may hold values from -96 to 96
- mode_table: bfloat16 [384, 1536], replicated, may hold values from -0.3125 to 0.3125
Outputs:
- update: bfloat16 [2, 384, 384, 384], P(None, 'mx', 'my', 'rep')
All inputs are finite; a program needn't handle non-finite values.
Results may differ from a plain program's by a relative error of at most 0.008.
Values may be sent and summed in bfloat16 or wider, within the bound.
A program may use at most 384 MiB of HBM per device.

v0:
```python
import jax
import jax.numpy as jnp
from jax import lax
from jax.sharding import PartitionSpec as P

DAMPING = 0.25


def body(coefficients, noise_field, mode_table):
    rep_index = lax.axis_index("rep")
    col_index = lax.axis_index("my")
    rep_count = lax.axis_size("rep")
    row_count = lax.axis_size("mx")
    col_count = lax.axis_size("my")
    planes_dev = noise_field.shape[0]
    planes_rep = planes_dev * row_count
    planes_all = planes_rep * rep_count
    mode_count = mode_table.shape[0]
    point_count = mode_table.shape[1]
    slab_first = point_count // 2 - planes_all // 2
    row_block = mode_count // row_count
    col_block = mode_count // col_count
    point_block = point_count // col_count
    own_block = mode_count // rep_count
    slab_own = lax.dynamic_slice_in_dim(
        mode_table, slab_first + rep_index * planes_rep, planes_rep, 1
    )
    zmodes = jnp.einsum(
        "pabk,kz->zpba", coefficients, slab_own, preferred_element_type=jnp.float32
    ).astype(jnp.bfloat16)
    zmodes = zmodes.reshape(planes_rep, 2, col_block * row_block)
    spread = lax.all_to_all(zmodes, "mx", split_axis=0, concat_axis=2, tiled=True)
    grouped = spread.reshape(planes_dev, 2, row_count, col_block, row_block)
    tiled_table = mode_table.reshape(row_count, row_block, point_count)
    own_points = lax.dynamic_slice_in_dim(tiled_table, col_index * point_block, point_block, 2)
    block_part = jnp.einsum(
        "zpsal,slx->zpax",
        lax.all_gather(grouped, "my", axis=3, tiled=True),
        own_points,
        preferred_element_type=jnp.float32,
    ).astype(jnp.bfloat16)
    wave_field = jnp.einsum(
        "zpax,ay->zpxy", block_part, mode_table, preferred_element_type=jnp.float32
    )
    wave_real = wave_field[:, 0]
    wave_imag = wave_field[:, 1]
    density = wave_real * wave_real + wave_imag * wave_imag
    noise_wide = noise_field.astype(jnp.float32)
    drive_term = jnp.stack(
        [
            density * (wave_imag - DAMPING * wave_real) + noise_wide[:, 0],
            density * (-wave_real - DAMPING * wave_imag) + noise_wide[:, 1],
        ],
        1,
    ).astype(jnp.bfloat16)
    proj_columns = jnp.einsum(
        "zpxy,ny->zpnx", drive_term, mode_table, preferred_element_type=jnp.float32
    ).astype(jnp.bfloat16)
    block_part = lax.all_to_all(proj_columns, "my", split_axis=2, concat_axis=3, tiled=True)
    folded = jnp.einsum(
        "zpax,slx->zpsal", block_part, tiled_table, preferred_element_type=jnp.float32
    ).astype(jnp.bfloat16)
    proj_rows = folded.reshape(
        block_part.shape[0], block_part.shape[1], row_count * col_block * row_block
    )
    gathered_rows = lax.all_to_all(proj_rows, "mx", split_axis=2, concat_axis=0, tiled=True)
    slab_back = lax.dynamic_slice_in_dim(mode_table, rep_index * own_block, own_block, 0)[
        :, slab_first : slab_first + planes_all
    ]
    portion = lax.all_gather(gathered_rows, "rep", axis=0, tiled=True)
    plane_grid = portion.reshape(portion.shape[0], 2, col_block, row_block)
    summed = jnp.einsum("zpba,nz->pabn", plane_grid, slab_back, preferred_element_type=jnp.float32)
    return summed.astype(jnp.bfloat16)


def solution(mesh):
    in_specs = (P(None, "mx", "my", None), P(("rep", "mx"), None, "my", None), P())
    out_specs = P(None, "mx", "my", "rep")
    return jax.shard_map(body, mesh=mesh, in_specs=in_specs, out_specs=out_specs, check_vma=False)
```

profile of v0, /device:TPU:0, one launch (start us, length us, event | category | flops | bytes accessed | tf_op | source)
XLA Modules:
  0.0 974.2 jit_solution(4171945368356783076)
XLA Ops:
  6.5 0.0 copy-start
  6.5 0.0 all-gather.3.cloned.1.call-start
  6.5 1.3 copy-done
  7.8 25.5 %convert_bitcast_fusion.3 = bf16[32,2,96,192]{2,0,3,1:T(8,128)(2,1)} fusion(bf16[2,192,96,384]{3,2,1,0:T(8,128)(2,1)} %param.3, bf16[384,1536]{1,0:T(8,128)(2,1)S(1)} %copy-done, s32[]{:T(128)S(6)} %select_n.10), kind=kOutput, calls=%fused_computation.17 | convolution fusion | flops 907149312 | bytes 30769156 | tf_op jit(solution)/shard_map/pabk,kz->zpba/dot_general | solution.py:28
  33.3 5.1 copy.45
  38.5 6.9 reshape.28
  45.3 31.8 %all_to_all.51 = bf16[32,2,18432]{2,1,0:T(2,128)(2,1)S(1)} all-to-all(bf16[32,2,18432]{2,1,0:T(2,128)(2,1)S(1)} %reshape.28), channel_id=1, replica_groups=mesh['rep'=4,'mx'=2,'my'=4] {'mx'}, dimensions={0} | all-to-all | bytes 4718592 | tf_op jit(solution)/shard_map/all_to_all | solution.py:32
  77.1 2.4 copy.52
  79.5 4.5 reshape.17
  84.0 0.0 all-gather.3.cloned.1.call-update
  84.0 0.2 all-gather.5.cloned.1.call-start
  84.2 37.8 %convert_element_type.34 = f32[16,2,384,1536]{3,2,1,0:T(8,128)} convert(bf16[16,2,384,1536]{3,2,1,0:T(8,128)(2,1)} %param.4) | non-fusion elementwise | flops 18874368 | bytes 113246208 | tf_op jit(solution)/shard_map/convert_element_type | solution.py:48
  122.1 180.8 %all-gather.3.cloned.1.call-done = bf16[16,2,2,384,192]{4,3,2,1,0:T(8,128)(2,1)} async-done(((bf16[16,2,2,96,192]{4,3,2,1,0:T(8,128)(2,1)}), bf16[16,2,2,384,192]{4,3,2,1,0:T(8,128)(2,1)}) %all-gather.3.cloned.1.call-update) | async-done | bytes 9437200 | tf_op jit(solution)/shard_map/all_gather | solution.py:38
  302.9 36.1 %fusion.6 = f32[16,2,384,1536]{3,2,1,0:T(8,128)} fusion(bf16[16,2,2,384,192]{4,3,2,1,0:T(8,128)(2,1)} %all-gather.3.cloned.1.call-done, bf16[384,1536]{1,0:T(8,128)(2,1)S(1)} %copy-done, bf16[2,192,1536]{2,1,0:T(8,128)(2,1)S(1)} %bitcast.69, s32[]{:T(128)S(6)} %select_n.11), kind=kOutput, calls=%fused_computation.10 | convolution fusion | flops 18124111872 | bytes 86409216 | tf_op jit(solution)/shard_map/zpax,ay->zpxy/dot_general | solution.py:42
  339.0 61.5 %fusion.1 = (bf16[16,1,384,1536]{3,2,1,0:T(8,128)(2,1)}, bf16[16,1,384,1536]{3,2,1,0:T(8,128)(2,1)}) fusion(f32[16,2,384,1536]{3,2,1,0:T(8,128)} %convert_element_type.34, f32[16,2,384,1536]{3,2,1,0:T(8,128)} %fusion.6), kind=kLoop, calls=%fused_computation.3 | loop fusion | flops 132120576 | bytes 188743680 | tf_op jit(solution)/shard_map/convert
  400.5 26.7 %convert_bitcast_fusion.1 = bf16[16,2,384,384]{2,3,1,0:T(8,128)(2,1)} fusion(bf16[16,1,384,1536]{3,2,1,0:T(8,128)(2,1)} %get-tuple-element.6, bf16[16,1,384,1536]{3,2,1,0:T(8,128)(2,1)} %get-tuple-element.5, bf16[384,1536]{1,0:T(8,128)(2,1)S(1)} %copy-done), kind=kOutput, calls=%fused_computation.15 | convolution fusion | flops 14519107584 | bytes 48365568 | tf_op jit(solution)/shard_map/zpxy,ny->zpnx/dot_general | solution.py:56
  427.2 23.9 %copy.29 = bf16[16,2,384,384]{3,1,0,2:T(2,128)(2,1)} copy(bf16[16,2,384,384]{2,3,1,0:T(8,128)(2,1)} %convert_bitcast_fusion.1) | data formatting | bytes 18874368 | tf_op jit(solution)/shard_map/convert_element_type | solution.py:58
  451.1 214.1 %all_to_all.52 = bf16[16,2,384,384]{3,1,0,2:T(2,128)(2,1)} all-to-all(bf16[16,2,384,384]{3,1,0,2:T(2,128)(2,1)} %copy.29), channel_id=1, replica_groups=mesh['rep'=4,'mx'=2,'my'=4] {'my'}, dimensions={2} | all-to-all | bytes 18874368 | tf_op jit(solution)/shard_map/all_to_all | solution.py:59
  665.3 10.9 %copy.30 = bf16[16,2,384,384]{3,2,1,0:T(8,128)(2,1)} copy(bf16[16,2,384,384]{3,1,0,2:T(2,128)(2,1)} %all_to_all.52) | data formatting | bytes 18874368 | tf_op jit(solution)/shard_map/all_to_all | solution.py:59
  676.2 10.6 %copy.31 = bf16[16,2,96,4,384]{4,3,2,1,0:T(4,128)(2,1)} copy(bf16[16,2,96,4,384]{4,2,3,1,0:T(8,128)(2,1)} %bitcast.73) | data formatting | bytes 18874368 | tf_op jit(solution)/shard_map/all_to_all | solution.py:59
  686.8 15.9 %reshape.25 = bf16[16,2,96,1536,1]{3,2,1,0,4:T(8,128)(2,1)} reshape(bf16[16,2,96,4,384]{4,3,2,1,0:T(4,128)(2,1)} %copy.31) | data formatting | bytes 18874368 | tf_op jit(solution)/shard_map/all_to_all | solution.py:59
  702.7 10.2 %convert_bitcast_fusion.2 = bf16[16,2,2,96,192]{4,3,2,1,0:T(8,128)(2,1)} fusion(bf16[2,192,1536,1,1]{2,1,0,4,3:T(8,128)(2,1)S(1)} %bitcast.68, bf16[16,2,96,1536,1]{3,2,1,0,4:T(8,128)(2,1)} %reshape.25), kind=kOutput, calls=%fused_computation.16 | convolution fusion | flops 3625058304 | bytes 12976128 | tf_op jit(solution)/shard_map/zpax,slx->zpsal/dot_general | solution.py:60
  712.8 35.2 %copy.46 = bf16[16,2,2,96,192]{0,1,4,3,2:T(2,128)(2,1)} copy(bf16[16,2,2,96,192]{4,3,2,1,0:T(8,128)(2,1)} %convert_bitcast_fusion.2) | data formatting | bytes 4718592 | tf_op jit(solution)/shard_map/reshape | solution.py:63
  748.1 27.3 %reshape.30 = bf16[2,2,294912]{2,1,0:T(2,128)(2,1)S(1)} reshape(bf16[36864,2,16]{2,1,0:T(2,128)(2,1)} %bitcast.70) | data formatting | bytes 4718592
  775.3 30.9 %all_to_all.53 = bf16[2,2,294912]{2,1,0:T(2,128)(2,1)} all-to-all(bf16[2,2,294912]{2,1,0:T(2,128)(2,1)S(1)} %reshape.30), channel_id=1, replica_groups=mesh['rep'=4,'mx'=2,'my'=4] {'mx'}, dimensions={0} | all-to-all | bytes 4718592 | tf_op jit(solution)/shard_map/all_to_all | solution.py:66
  806.2 22.4 %reshape.31 = bf16[36864,2,16]{2,1,0:T(2,128)(2,1)} reshape(bf16[2,2,294912]{2,1,0:T(2,128)(2,1)} %all_to_all.53) | data formatting | bytes 4718592
  828.6 35.6 %copy.34 = bf16[2,16,2,18432]{3,1,0,2:T(8,128)(2,1)} copy(bf16[2,16,2,18432]{1,2,3,0:T(2,128)(2,1)} %bitcast.71) | data formatting | bytes 4718592 | tf_op jit(solution)/shard_map/all_to_all | solution.py:66
  864.2 0.0 all-gather.5.cloned.1.call-update
  864.2 62.8 %all-gather.5.cloned.1.call-done = bf16[128,2,18432]{2,0,1:T(8,128)(2,1)} async-done(((bf16[32,2,18432]{2,0,1:T(8,128)(2,1)}), bf16[128,2,18432]{2,0,1:T(8,128)(2,1)}) %all-gather.5.cloned.1.call-update) | async-done | bytes 9437200 | tf_op jit(solution)/shard_map/all_gather | solution.py:70
  927.0 12.6 %copy.35 = bf16[128,2,18432]{0,2,1:T(8,128)(2,1)} copy(bf16[128,2,18432]{2,0,1:T(8,128)(2,1)} %all-gather.5.cloned.1.call-done) | data formatting | bytes 18874368 | tf_op jit(solution)/shard_map/all_gather | solution.py:70
  939.6 13.8 %convert_bitcast_fusion = bf16[2,192,96,96]{1,3,2,0:T(8,128)(2,1)} fusion(bf16[128,2,96,192]{0,3,2,1:T(8,128)(2,1)} %bitcast.72, bf16[384,1536]{1,0:T(8,128)(2,1)S(1)} %copy-done, s32[]{:T(128)S(6)} %select_n.9, s32[]{:T(128)S(6)} %add.30), kind=kOutput, calls=%fused_computation.14 | convolution fusion | flops 909508608 | bytes 16539656 | tf_op jit(solution)/shard_map/zpba,nz->pabn/dot_general | solution.py:72
  953.3 13.9 %copy.36 = bf16[2,192,96,96]{3,2,1,0:T(8,128)(2,1)} copy(bf16[2,192,96,96]{1,3,2,0:T(8,128)(2,1)} %convert_bitcast_fusion) | data formatting | bytes 14155776 | tf_op jit(solution)/shard_map/convert_element_type | solution.py:73
Async XLA Ops:
  6.5 1.3 copy-start
  6.5 296.3 %all-gather.3.cloned.1.call-start = ((), (), s32[]{:S(2)}) async-start(), calls=%async_computation.3 | async-start | bytes 15728640 | tf_op jit(solution)/shard_map/all_gather | solution.py:38
  84.0 843.0 %all-gather.5.cloned.1.call-start = ((), (), s32[]{:S(2)}) async-start(), calls=%async_computation.4 | async-start | bytes 11796480 | tf_op jit(solution)/shard_map/all_gather | solution.py:70
Sparse Core Ops, SparseCore 0:
  84.1 218.6 all-gather.2
  864.3 62.6 all-gather.4
where the time goes:
time: 986 us; the launch traced here: 974 us
  blocking collectives  277 us (28%)
  waiting for transfers between devices  244 us (25%)
  local copies, waits for them, and re-layouts  228 us (23%)
  matrix products  112 us (11%)
  other arithmetic  99.4 us (10%)
  between operations  13.6 us (1%)
    all_to_all x1, blocking collectives, body(): lax.all_to_all(proj_columns, 'my', split_axis=2, concat_axis=3, tiled=True)  214 us
    all_gather x1, waiting for transfers between devices, body(): lax.all_gather(grouped, 'my', axis=3, tiled=True)  181 us
    all_gather x1, waiting for transfers between devices, body(): portion = lax.all_gather(gathered_rows, 'rep', axis=0, tiled=True)  62.8 us
    another operation x1, other arithmetic  61.5 us
    unnamed x4, local copies, waits for them, and re-layouts  50.9 us
    convert_element_type x1, other arithmetic, body(): noise_wide = noise_field.astype(jnp.float32)  37.8 us
    all_to_all x3, local copies, waits for them, and re-layouts, body(): lax.all_to_all(proj_columns, 'my', split_axis=2, concat_axis=3, tiled=True)  37.4 us
    dot_general x1, matrix products, body(): jnp.einsum('zpax,ay->zpxy', block_part, mode_table, preferred_element_typ...  36.1 us
  transfers between devices with their start and end apart: 2, of which 2 were waited for; matrix products, arithmetic and copies ran while one was open for 4% of the time, Pallas kernels for 0%

commit v1 on v0

--- a/solution.py
+++ b/solution.py
@@ -67,7 +67,22 @@
     slab_back = lax.dynamic_slice_in_dim(mode_table, rep_index * own_block, own_block, 0)[
         :, slab_first : slab_first + planes_all
     ]
-    portion = lax.all_gather(gathered_rows, "rep", axis=0, tiled=True)
+
+    def change_the_figure(lane_axis, arr):
+        fan = lax.axis_size(lane_axis)
+        arrivals = [(k0, (k0 + 1) % fan) for k0 in range(fan)]
+
+        def _remake_slices(later):
+            if len(later) == fan:
+                return later
+            r2 = _remake_slices([lax.ppermute(later[0], lane_axis, arrivals), *later])
+            return r2
+
+        w2 = jnp.concatenate(_remake_slices([arr]), 0)
+        near = jnp.roll(w2, (lax.axis_index(lane_axis) + 1) * arr.shape[0], 0)
+        return near
+
+    portion = change_the_figure("rep", gathered_rows)
     plane_grid = portion.reshape(portion.shape[0], 2, col_block, row_block)
     summed = jnp.einsum("zpba,nz->pabn", plane_grid, slab_back, preferred_element_type=jnp.float32)
     return summed.astype(jnp.bfloat16)

time: 986 us -> 1040 us (1.055)
  local copies, waits for them, and re-layouts: 228 us -> 258 us
  waiting for transfers between devices: 244 us -> 266 us
    ppermute x0 -> x3, waiting for transfers between devices: none -> 85.2 us  [_remake_slices(): r2 = _remake_slices([lax.ppermute(later[0], lane_axis, arrivals), *later])]
    all_gather x1 -> x0, waiting for transfers between devices: 62.8 us -> none  [body(): portion = lax.all_gather(gathered_rows, 'rep', axis=0, tiled=True)]
    dynamic_slice x0 -> x2, local copies, waits for them, and re-layouts: none -> 21.3 us  [change_the_figure(): near = jnp.roll(w2, (lax.axis_index(lane_axis) + 1) * arr.shape[0], 0)]
    unnamed x4 -> x15, local copies, waits for them, and re-layouts: 50.9 us -> 71.4 us
    all_gather x1 -> x0, local copies, waits for them, and re-layouts: 12.6 us -> none  [body(): portion = lax.all_gather(gathered_rows, 'rep', axis=0, tiled=True)]
  transfers between devices with their start and end apart: 2 -> 4, of which waited for: 2 -> 4; matrix products, arithmetic and copies ran while one was open for 4% -> 4% of each run, Pallas kernels for 0% -> 0%
where the time goes in v1:
time: 1040 us; the launch traced here: 1030 us
  blocking collectives  277 us (27%)
  waiting for transfers between devices  266 us (26%)
  local copies, waits for them, and re-layouts  258 us (25%)
  matrix products  112 us (11%)
  other arithmetic  99.5 us (10%)
  between operations  13.7 us (1%)
    all_to_all x1, blocking collectives, body(): lax.all_to_all(proj_columns, 'my', split_axis=2, concat_axis=3, tiled=True)  214 us
    all_gather x1, waiting for transfers between devices, body(): lax.all_gather(grouped, 'my', axis=3, tiled=True)  181 us
    ppermute x3, waiting for transfers between devices, _remake_slices(): r2 = _remake_slices([lax.ppermute(later[0], lane_axis, arrivals), *later])  85.2 us
    unnamed x15, local copies, waits for them, and re-layouts  71.4 us
    another operation x1, other arithmetic  61.6 us
    convert_element_type x1, other arithmetic, body(): noise_wide = noise_field.astype(jnp.float32)  38 us
    all_to_all x3, local copies, waits for them, and re-layouts, body(): lax.all_to_all(proj_columns, 'my', split_axis=2, concat_axis=3, tiled=True)  37.3 us
    dot_general x1, matrix products, body(): jnp.einsum('zpax,ay->zpxy', block_part, mode_table, preferred_element_typ...  36.1 us
  transfers between devices with their start and end apart: 4, of which 4 were waited for; matrix products, arithmetic and copies ran while one was open for 4% of the time, Pallas kernels for 0%

profile of v1, /device:TPU:0, one launch (start us, length us, event | category | flops | bytes accessed | tf_op | source)
XLA Modules:
  0.0 1026.5 jit_solution(9667089754857323255)
XLA Ops:
  6.5 0.0 copy-start
  6.5 0.0 all-gather.2.cloned.1.call-start
  6.5 1.3 copy-done
  7.8 25.5 %convert_bitcast_fusion.3 = bf16[32,2,96,192]{2,0,3,1:T(8,128)(2,1)} fusion(bf16[2,192,96,384]{3,2,1,0:T(8,128)(2,1)} %param.3, bf16[384,1536]{1,0:T(8,128)(2,1)S(1)} %copy-done, s32[]{:T(128)S(6)} %select_n.23), kind=kOutput, calls=%fused_computation.17 | convolution fusion | flops 907149312 | bytes 30769156 | tf_op jit(solution)/shard_map/pabk,kz->zpba/dot_general | solution.py:28
  33.3 5.1 copy.45
  38.5 6.9 reshape.28
  45.3 31.9 %all_to_all.51 = bf16[32,2,18432]{2,1,0:T(2,128)(2,1)S(1)} all-to-all(bf16[32,2,18432]{2,1,0:T(2,128)(2,1)S(1)} %reshape.28), channel_id=1, replica_groups=mesh['rep'=4,'mx'=2,'my'=4] {'mx'}, dimensions={0} | all-to-all | bytes 4718592 | tf_op jit(solution)/shard_map/all_to_all | solution.py:32
  77.2 2.4 copy.52
  79.7 4.5 reshape.17
  84.1 0.0 all-gather.2.cloned.1.call-update
  84.2 38.0 %convert_element_type.34 = f32[16,2,384,1536]{3,2,1,0:T(8,128)} convert(bf16[16,2,384,1536]{3,2,1,0:T(8,128)(2,1)} %param.4) | non-fusion elementwise | flops 18874368 | bytes 113246208 | tf_op jit(solution)/shard_map/convert_element_type | solution.py:48
  122.1 180.9 %all-gather.2.cloned.1.call-done = bf16[16,2,2,384,192]{4,3,2,1,0:T(8,128)(2,1)} async-done(((bf16[16,2,2,96,192]{4,3,2,1,0:T(8,128)(2,1)}), bf16[16,2,2,384,192]{4,3,2,1,0:T(8,128)(2,1)}) %all-gather.2.cloned.1.call-update) | async-done | bytes 9437200 | tf_op jit(solution)/shard_map/all_gather | solution.py:38
  303.0 36.1 %fusion.6 = f32[16,2,384,1536]{3,2,1,0:T(8,128)} fusion(bf16[16,2,2,384,192]{4,3,2,1,0:T(8,128)(2,1)} %all-gather.2.cloned.1.call-done, bf16[384,1536]{1,0:T(8,128)(2,1)S(1)} %copy-done, bf16[2,192,1536]{2,1,0:T(8,128)(2,1)S(1)} %bitcast.69, s32[]{:T(128)S(6)} %select_n.24), kind=kOutput, calls=%fused_computation.10 | convolution fusion | flops 18124111872 | bytes 86409216 | tf_op jit(solution)/shard_map/zpax,ay->zpxy/dot_general | solution.py:42
  339.1 61.6 %fusion.1 = (bf16[16,1,384,1536]{3,2,1,0:T(8,128)(2,1)}, bf16[16,1,384,1536]{3,2,1,0:T(8,128)(2,1)}) fusion(f32[16,2,384,1536]{3,2,1,0:T(8,128)} %convert_element_type.34, f32[16,2,384,1536]{3,2,1,0:T(8,128)} %fusion.6), kind=kLoop, calls=%fused_computation.3 | loop fusion | flops 132120576 | bytes 188743680 | tf_op jit(solution)/shard_map/convert
  400.7 26.5 %convert_bitcast_fusion.1 = bf16[16,2,384,384]{2,3,1,0:T(8,128)(2,1)} fusion(bf16[16,1,384,1536]{3,2,1,0:T(8,128)(2,1)} %get-tuple-element.6, bf16[16,1,384,1536]{3,2,1,0:T(8,128)(2,1)} %get-tuple-element.5, bf16[384,1536]{1,0:T(8,128)(2,1)S(1)} %copy-done), kind=kOutput, calls=%fused_computation.15 | convolution fusion | flops 14519107584 | bytes 48365568 | tf_op jit(solution)/shard_map/zpxy,ny->zpnx/dot_general | solution.py:56
  427.2 23.9 %copy.29 = bf16[16,2,384,384]{3,1,0,2:T(2,128)(2,1)} copy(bf16[16,2,384,384]{2,3,1,0:T(8,128)(2,1)} %convert_bitcast_fusion.1) | data formatting | bytes 18874368 | tf_op jit(solution)/shard_map/convert_element_type | solution.py:58
  451.1 214.3 %all_to_all.52 = bf16[16,2,384,384]{3,1,0,2:T(2,128)(2,1)} all-to-all(bf16[16,2,384,384]{3,1,0,2:T(2,128)(2,1)} %copy.29), channel_id=1, replica_groups=mesh['rep'=4,'mx'=2,'my'=4] {'my'}, dimensions={2} | all-to-all | bytes 18874368 | tf_op jit(solution)/shard_map/all_to_all | solution.py:59
  665.4 10.9 %copy.30 = bf16[16,2,384,384]{3,2,1,0:T(8,128)(2,1)} copy(bf16[16,2,384,384]{3,1,0,2:T(2,128)(2,1)} %all_to_all.52) | data formatting | bytes 18874368 | tf_op jit(solution)/shard_map/all_to_all | solution.py:59
  676.3 10.5 %copy.31 = bf16[16,2,96,4,384]{4,3,2,1,0:T(4,128)(2,1)} copy(bf16[16,2,96,4,384]{4,2,3,1,0:T(8,128)(2,1)} %bitcast.73) | data formatting | bytes 18874368 | tf_op jit(solution)/shard_map/all_to_all | solution.py:59
  686.8 15.9 %reshape.25 = bf16[16,2,96,1536,1]{3,2,1,0,4:T(8,128)(2,1)} reshape(bf16[16,2,96,4,384]{4,3,2,1,0:T(4,128)(2,1)} %copy.31) | data formatting | bytes 18874368 | tf_op jit(solution)/shard_map/all_to_all | solution.py:59
  702.7 10.1 convert_bitcast_fusion.2
  712.8 35.3 %copy.46 = bf16[16,2,2,96,192]{0,1,4,3,2:T(2,128)(2,1)} copy(bf16[16,2,2,96,192]{4,3,2,1,0:T(8,128)(2,1)} %convert_bitcast_fusion.2) | data formatting | bytes 4718592 | tf_op jit(solution)/shard_map/reshape | solution.py:63
  748.1 27.0 %reshape.30 = bf16[2,2,294912]{2,1,0:T(2,128)(2,1)S(1)} reshape(bf16[36864,2,16]{2,1,0:T(2,128)(2,1)} %bitcast.70) | data formatting | bytes 4718592
  775.1 30.9 %all_to_all.53 = bf16[2,2,294912]{2,1,0:T(2,128)(2,1)} all-to-all(bf16[2,2,294912]{2,1,0:T(2,128)(2,1)S(1)} %reshape.30), channel_id=1, replica_groups=mesh['rep'=4,'mx'=2,'my'=4] {'mx'}, dimensions={0} | all-to-all | bytes 4718592 | tf_op jit(solution)/shard_map/all_to_all | solution.py:66
  806.0 22.4 %reshape.31 = bf16[36864,2,16]{2,1,0:T(2,128)(2,1)} reshape(bf16[2,2,294912]{2,1,0:T(2,128)(2,1)} %all_to_all.53) | data formatting | bytes 4718592
  828.4 34.3 %copy.34 = bf16[2,16,2,18432]{3,1,0,2:T(8,128)(2,1)S(1)} copy(bf16[2,16,2,18432]{1,2,3,0:T(2,128)(2,1)} %bitcast.71) | data formatting | bytes 4718592 | tf_op jit(solution)/shard_map/all_to_all | solution.py:66
  862.7 0.1 collective-permute-start
  862.8 28.3 %collective-permute-done = bf16[32,2,18432]{2,0,1:T(8,128)(2,1)S(1)} collective-permute-done((bf16[32,2,18432]{2,0,1:T(8,128)(2,1)S(1)}, bf16[32,2,18432]{2,0,1:T(8,128)(2,1)S(1)}, u32[]{:S(2)}, u32[]{:S(2)}) %collective-permute-start) | collective-permute-done | bytes 2359328 | tf_op jit(solution)/shard_map/ppermute | solution.py:78
  891.0 0.0 copy-start.1
  891.0 1.4 copy-done.1
  892.4 0.0 collective-permute-start.1
  892.4 28.4 %collective-permute-done.1 = bf16[32,2,18432]{2,0,1:T(8,128)(2,1)} collective-permute-done((bf16[32,2,18432]{2,0,1:T(8,128)(2,1)S(1)}, bf16[32,2,18432]{2,0,1:T(8,128)(2,1)}, u32[]{:S(2)}, u32[]{:S(2)}) %collective-permute-start.1) | collective-permute-done | bytes 2359328 | tf_op jit(solution)/shard_map/ppermute | solution.py:78
  920.8 0.0 collective-permute-start.2
  920.8 0.0 copy-start.2
  920.8 28.6 %collective-permute-done.2 = bf16[32,2,18432]{2,0,1:T(8,128)(2,1)} collective-permute-done((bf16[32,2,18432]{2,0,1:T(8,128)(2,1)}, bf16[32,2,18432]{2,0,1:T(8,128)(2,1)}, u32[]{:S(2)}, u32[]{:S(2)}) %collective-permute-start.2) | collective-permute-done | bytes 2359328 | tf_op jit(solution)/shard_map/ppermute | solution.py:78
  949.4 3.3 constant_dynamic-update-slice_fusion.7
  952.6 3.3 constant_dynamic-update-slice_fusion.6
  955.9 3.2 constant_dynamic-update-slice_fusion.5
  959.1 1.5 constant_dynamic-update-slice_fusion.4
  960.7 3.2 constant_dynamic-update-slice_fusion.3
  963.9 3.2 constant_dynamic-update-slice_fusion.2
  967.1 0.0 copy-done.2
  967.1 1.6 constant_dynamic-update-slice_fusion.1
  968.8 1.6 constant_dynamic-update-slice_fusion
  970.4 8.4 constant_dynamic-slice_fusion
  978.8 12.9 %copy.35 = bf16[128,2,18432]{0,2,1:T(8,128)(2,1)} copy(bf16[128,2,18432]{2,0,1:T(8,128)(2,1)} %constant_dynamic-slice_fusion) | data formatting | bytes 18874368 | tf_op jit(solution)/shard_map/jit(_roll_dynamic)/dynamic_slice | solution.py:82
  991.7 13.8 %convert_bitcast_fusion = bf16[2,192,96,96]{1,3,2,0:T(8,128)(2,1)} fusion(bf16[128,2,96,192]{0,3,2,1:T(8,128)(2,1)} %bitcast.72, bf16[384,1536]{1,0:T(8,128)(2,1)S(1)} %copy-done, s32[]{:T(128)S(6)} %select_n.22, s32[]{:T(128)S(6)} %add.46), kind=kOutput, calls=%fused_computation.14 | convolution fusion | flops 909508608 | bytes 16539656 | tf_op jit(solution)/shard_map/zpba,nz->pabn/dot_general | solution.py:87
  1005.5 13.9 %copy.36 = bf16[2,192,96,96]{3,2,1,0:T(8,128)(2,1)} copy(bf16[2,192,96,96]{1,3,2,0:T(8,128)(2,1)} %convert_bitcast_fusion) | data formatting | bytes 14155776 | tf_op jit(solution)/shard_map/convert_element_type | solution.py:88
Async XLA Ops:
  6.5 1.3 copy-start
  6.5 296.5 %all-gather.2.cloned.1.call-start = ((), (), s32[]{:S(2)}) async-start(), calls=%async_computation.3 | async-start | bytes 15728640 | tf_op jit(solution)/shard_map/all_gather | solution.py:38
  862.7 28.3 %collective-permute-start = (bf16[32,2,18432]{2,0,1:T(8,128)(2,1)S(1)}, bf16[32,2,18432]{2,0,1:T(8,128)(2,1)S(1)}, u32[]{:S(2)}, u32[]{:S(2)}) collective-permute-start(bf16[32,2,18432]{2,0,1:T(8,128)(2,1)S(1)} %bitcast.74), channel_id=1, source_target_pairs={{0,8},{8,16},{16,24},{24,0},{1,9},{9,17},{17,25},{25,1},{2,10},{10... | collective-permute-start | bytes 7077896 | tf_op jit(solution)/shard_map/ppermute | solution.py:78
  891.0 1.4 copy-start.1
  892.4 28.4 %collective-permute-start.1 = (bf16[32,2,18432]{2,0,1:T(8,128)(2,1)S(1)}, bf16[32,2,18432]{2,0,1:T(8,128)(2,1)}, u32[]{:S(2)}, u32[]{:S(2)}) collective-permute-start(bf16[32,2,18432]{2,0,1:T(8,128)(2,1)S(1)} %collective-permute-done), channel_id=1, source_target_pairs={{0,8},{8,16},{16,24},{24,0},{1,9},{9,17},{17,25},{25,1},{2,10},{10... | collective-permute-start | bytes 7077896 | tf_op jit(solution)/shard_map/ppermute | solution.py:78
  920.8 28.6 %collective-permute-start.2 = (bf16[32,2,18432]{2,0,1:T(8,128)(2,1)}, bf16[32,2,18432]{2,0,1:T(8,128)(2,1)}, u32[]{:S(2)}, u32[]{:S(2)}) collective-permute-start(bf16[32,2,18432]{2,0,1:T(8,128)(2,1)} %collective-permute-done.1), channel_id=1, source_target_pairs={{0,8},{8,16},{16,24},{24,0},{1,9},{9,17},{17,25},{25,1},{2,10},{10... | collective-permute-start | bytes 7077896 | tf_op jit(solution)/shard_map/ppermute | solution.py:78
  920.8 46.3 %copy-start.2 = (bf16[32,2,18432]{2,0,1:T(8,128)(2,1)S(1)}, bf16[32,2,18432]{2,0,1:T(8,128)(2,1)}, u32[]{:S(2)}) copy-start(bf16[32,2,18432]{2,0,1:T(8,128)(2,1)} %copy-done.1) | copy-start | bytes 7077892
Sparse Core Ops, SparseCore 0:
  84.3 218.6 all-gather.1
